TPU v7x, 128 devices: a whole 4x4x4 slice. The times are simulated.
128 devices in a mesh: row: 8 (over z, core), col: 16 (over y, x).
Axes of the slice: x: 4, y: 4, z: 4, core: 2. Of those that a mesh axis runs over, the one named last changes fastest.
Arguments:
- inverse_interior: float32 [8, 16, 1536, 1536], P('row', 'col'), may hold values from -0.15625 to 0.15625
- coupling: float32 [8, 16, 1536, 1024], P('row', 'col'), may hold values from -1 to 1
- interface_block: float32 [8, 16, 1024, 1024], P('row', 'col'), may hold values from -6 to 6
- iface_ids: int32 [8, 16, 4], P('row', 'col'), may hold values from 0 to 15, as said below
- row_place: int32 [16], replicated, may hold values from 0 to 15, as said below
- col_place: int32 [16], replicated, may hold values from 0 to 15, as said below
Outputs:
- assembled: float32 [16, 256, 16, 256], P('row', None, 'col')
Inputs may be any that keep to these rules, and one draw needn't show every extreme that they name: `row_place`: A permutation of the tile ids. `col_place`: a permutation of the tile ids; two ids whose values of row_place differ mod 8 have values of col_place that differ mod 16. `iface_ids`: the 4 ids of one subdomain have pairwise different row_place mod 8, hence pairwise different col_place mod 16.
All inputs are finite; a program needn't handle non-finite values.
Results may differ from a plain program's by a relative error of at most 0.0001.
Values sent between devices are 32-bit elements; how exact they have to be, the bound alone decides.
A program may use at most 192 MiB of HBM per device.

v0:
```python
import functools

import jax
import jax.numpy as jnp
from jax import lax
from jax.experimental import pallas as pl
from jax.experimental.pallas import tpu as pltpu
from jax.sharding import PartitionSpec as P

TILE = 256
MESH = pl.DeviceIdType.MESH

ORDER = (
    (0, 1), (1, 0), (0, 3), (3, 0), (0, 2), (2, 0), (1, 1), (3, 3),
    (1, 3), (3, 1), (1, 2), (2, 1), (2, 3), (3, 2), (2, 2),
)
ROTATION = (0, 0, 0, 0)


def plane_of(r, z, y, x):
    return ((y, x, z), (z, y, x), (x, z, y))[r]


def chip_of(r, u, v, w):
    return ((w, u, v), (u, v, w), (v, w, u))[r]


def kernel(pieces, table, out, arrived0, arrived1, arrived2, arrived3, table_in, table_s, give, take, grid, moved, done, final, zero_sem,
           data_s, data_r, tab_s, tab_r, own_sem, sib_s, sib_r, mov_s, mov_r, fin_s, fin_r):
    row, col = lax.axis_index("row"), lax.axis_index("col")
    z, core = row // 2, row % 2
    y, x = col // 4, col % 4
    arrived = (arrived0, arrived1, arrived2, arrived3)
    chunks = range(len(ROTATION))
    rotations = sorted(set(ROTATION))

    def device(zz, yy, xx, cc=None):
        return (zz * 2 + (core if cc is None else cc), yy * 4 + xx)

    def member(r, du, dv, dw=0):
        u, v, w = plane_of(r, z, y, x)
        return device(*chip_of(r, (u + du) % 4, (v + dv) % 4, (w + dw) % 4))

    def place(r, du=0, dv=0):
        u, v, _ = plane_of(r, z, y, x)
        return ((u + du) % 4) * 4 + (v + dv) % 4

    sibling = device(z, y, x, 1 - core)

    offsets = set()
    for r in rotations:
        for du, dv in ORDER:
            offsets.add(chip_of(r, du, dv, 0))
        for dw in (1, 2, 3):
            offsets.add(chip_of(r, 0, 0, dw))
    offsets = sorted(offsets)
    barrier = pltpu.get_barrier_semaphore()
    for dz, dy, dx in offsets:
        pl.semaphore_signal(barrier, inc=1, device_id=device((z + dz) % 4, (y + dy) % 4, (x + dx) % 4),
                            device_id_type=MESH)
    pl.semaphore_signal(barrier, inc=1, device_id=sibling, device_id_type=MESH)

    for c in chunks:
        arrived[c][:, 4, :] = jnp.zeros((16, 5, 8, 128), jnp.float32)
        arrived[c][:, :, 4] = jnp.zeros((16, 5, 8, 128), jnp.float32)
    pl.semaphore_wait(barrier, len(offsets) + 1)

    waits = []
    table_copies, data_copies = {}, {}
    for n, r in enumerate(rotations):
        for k, (du, dv) in enumerate(ORDER):
            copy = pltpu.make_async_remote_copy(
                src_ref=table, dst_ref=table_in.at[n, place(r)], send_sem=tab_s.at[n, k],
                recv_sem=tab_r.at[n, k], device_id=member(r, du, dv), device_id_type=MESH)
            copy.start()
            table_copies[n, k] = copy
    for c in chunks:
        r = ROTATION[c]
        for k, (du, dv) in enumerate(ORDER):
            copy = pltpu.make_async_remote_copy(
                src_ref=pieces.at[c, place(r, du, dv)], dst_ref=arrived[c].at[place(r), pl.ds(0, 4), pl.ds(0, 4)],
                send_sem=data_s.at[c, k], recv_sem=data_r.at[c, k],
                device_id=member(r, du, dv), device_id_type=MESH)
            copy.start()
            data_copies[c, k] = copy
    own_copies = []
    for c in chunks:
        p = place(ROTATION[c])
        copy = pltpu.make_async_copy(pieces.at[c, p], arrived[c].at[p, pl.ds(0, 4), pl.ds(0, 4)], own_sem.at[c])
        copy.start()
        own_copies.append(copy)
    for n, r in enumerate(rotations):
        table_in[n, place(r)] = table[...]
    for n, r in enumerate(rotations):
        for k in range(15):
            table_copies[n, k].wait()
        copy = pltpu.make_async_copy(table_in.at[n], table_s.at[n], zero_sem)
        copy.start()
        copy.wait()

    sib_copies, mov_copies, fin_copies = {}, {}, {}

    def reduce(c, target, who):
        r = ROTATION[c]
        n = rotations.index(r)

        def body(zz, carry):
            first = zz * 4 + who * 2
            acc = [[None] * 16 for _ in range(2)]
            for s in range(16):
                ra = [table_s[n, s, 0, first + slot] for slot in range(2)]
                for j in range(16):
                    cb = table_s[n, s, 0, 16 + j]
                    for slot in range(2):
                        block = arrived[c][s, ra[slot], cb]
                        acc[slot][j] = block if s == 0 else acc[slot][j] + block
            for j in range(16):
                u, v, w = plane_of(r, zz, j // 4, j % 4)
                for slot in range(2):
                    target[c, w, u * 4 + v, slot] = acc[slot][j]
            return carry

        lax.fori_loop(0, 4, body, 0)

    def stage_reduce(c):
        for k in range(15):
            data_copies[c, k].wait_recv()
        own_copies[c].wait()
        reduce(c, give, 1 - core)
        copy = pltpu.make_async_remote_copy(
            src_ref=give.at[c], dst_ref=take.at[c], send_sem=sib_s.at[c], recv_sem=sib_r.at[c],
            device_id=sibling, device_id_type=MESH)
        copy.start()
        sib_copies[c] = copy
        reduce(c, grid, core)

    def stage_move(c):
        r = ROTATION[c]
        _, _, w = plane_of(r, z, y, x)
        sib_copies[c].wait_recv()
        for dw in (2, 1, 3, 0):
            there = (w + dw) % 4
            grid[c, there] = grid[c, there] + take[c, there]
            if dw:
                copy = pltpu.make_async_remote_copy(
                    src_ref=grid.at[c, there], dst_ref=moved.at[c, dw - 1], send_sem=mov_s.at[c, dw - 1],
                    recv_sem=mov_r.at[c, dw - 1], device_id=member(r, 0, 0, dw), device_id_type=MESH)
                copy.start()
                mov_copies[c, dw] = copy

    def stage_final(c):
        r = ROTATION[c]
        _, _, w = plane_of(r, z, y, x)
        h, q = c // 2, c % 2
        for dw in (1, 2, 3):
            mov_copies[c, dw].wait_recv()
        done[c] = grid[c, w] + moved[c, 0] + moved[c, 1] + moved[c, 2]
        p = place(r)
        rows = pl.ds(pl.multiple_of(q * 128 + p * 8, 8), 8)
        for k, (du, dv) in enumerate(ORDER):
            copy = pltpu.make_async_remote_copy(
                src_ref=done.at[c, place(r, du, dv)], dst_ref=final.at[:, rows, pl.ds(h * 128, 128)],
                send_sem=fin_s.at[c, k], recv_sem=fin_r.at[c, k],
                device_id=member(r, du, dv), device_id_type=MESH)
            copy.start()
            fin_copies[c, k] = copy
        final[:, rows, h * 128:(h + 1) * 128] = done[c, p]

    last = len(ROTATION) - 1
    for step in range(last + 3):
        if step <= last:
            stage_reduce(step)
        if 0 <= step - 1 <= last:
            stage_move(step - 1)
        if 0 <= step - 2 <= last:
            stage_final(step - 2)
    for c in chunks:
        for k in range(15):
            fin_copies[c, k].wait_recv()
    out[...] = final[...]
    for c in chunks:
        for k in range(15):
            data_copies[c, k].wait_send()
            fin_copies[c, k].wait_send()
        for dw in (1, 2, 3):
            mov_copies[c, dw].wait_send()
        sib_copies[c].wait_send()


def on_device(inverse_interior, coupling, interface_block, iface_ids, row_place, col_place):
    high = lax.Precision.HIGH
    solved = jnp.dot(inverse_interior[0, 0], coupling[0, 0], precision=high, preferred_element_type=jnp.float32)
    product = lax.dot_general(coupling[0, 0], solved, (((0,), (0,)), ((), ())), precision=high,
                              preferred_element_type=jnp.float32)
    schur = interface_block[0, 0] - product
    pieces = schur.reshape(4, 2, 16, 8, 4, 2, 128).transpose(5, 1, 2, 0, 4, 3, 6).reshape(4, 16, 4, 4, 8, 128)
    ids = iface_ids[0, 0]
    rowpos = (row_place % 8) * 2 + row_place // 8
    matches = ids[:, None] == jnp.arange(16, dtype=jnp.int32)[None, :]
    rows = jnp.sum(jnp.where(matches, rowpos[None, :], 0), axis=1)
    cols = jnp.sum(jnp.where(matches, col_place[None, :], 0), axis=1)
    lane = jnp.arange(128, dtype=jnp.int32)
    wanted = jnp.concatenate([rows, cols + 16]).astype(jnp.int32)
    value = jnp.tile(jnp.arange(4, dtype=jnp.int32), 2)
    hit = wanted[:, None] == lane[None, :]
    table = jnp.where(jnp.any(hit, axis=0), jnp.sum(jnp.where(hit, value[:, None], 0), axis=0), 4)[None, :]
    chunks, planes = len(ROTATION), len(set(ROTATION))
    f32 = jnp.float32
    vmem = pl.BlockSpec(memory_space=pltpu.VMEM)
    dma = pltpu.SemaphoreType.DMA
    out = pl.pallas_call(
        kernel,
        out_shape=jax.ShapeDtypeStruct((2, 256, 256), f32),
        in_specs=[pl.BlockSpec(memory_space=pl.ANY), vmem],
        out_specs=vmem,
        scratch_shapes=[
            *[pltpu.VMEM((16, 5, 5, 8, 128), f32)] * chunks,
            pltpu.VMEM((planes, 16, 1, 128), jnp.int32),
            pltpu.SMEM((planes, 16, 1, 128), jnp.int32),
            pltpu.VMEM((chunks, 4, 16, 2, 8, 128), f32),
            pltpu.VMEM((chunks, 4, 16, 2, 8, 128), f32),
            pltpu.VMEM((chunks, 4, 16, 2, 8, 128), f32),
            pltpu.VMEM((chunks, 3, 16, 2, 8, 128), f32),
            pltpu.VMEM((chunks, 16, 2, 8, 128), f32),
            pltpu.VMEM((2, 256, 256), f32),
            dma,
            dma((chunks, 15)), dma((chunks, 15)),
            dma((planes, 15)), dma((planes, 15)),
            dma((chunks,)),
            dma((chunks,)), dma((chunks,)),
            dma((chunks, 3)), dma((chunks, 3)),
            dma((chunks, 15)), dma((chunks, 15)),
        ],
        compiler_params=pltpu.CompilerParams(collective_id=0, has_side_effects=True, vmem_limit_bytes=48 * 2**20),
    )(pieces, table)
    return out[:, :, None, :]


def solution(mesh):
    return jax.shard_map(
        on_device,
        mesh=mesh,
        in_specs=(
            P("row", "col", None, None),
            P("row", "col", None, None),
            P("row", "col", None, None),
            P("row", "col", None),
            P(),
            P(),
        ),
        out_specs=P("row", None, "col", None),
        check_vma=False,
    )
```

profile of v0, /device:TPU:0, one launch (start us, length us, event | category | flops | bytes accessed | tf_op | source)
XLA Modules:
  0.0 131.9 jit_solution(17543130347982523932)
XLA Ops:
  0.0 0.0 slice-start
  0.0 5.5 %copy.14 = f32[1,1,1024,1024]{2,3,1,0:T(8,128)} copy(f32[1,1,1024,1024]{3,2,1,0:T(8,128)} %param.8) | data formatting | bytes 8388608 | tf_op args[2]
  5.5 0.0 copy-start.1
  5.5 0.0 slice-start.1
  5.5 18.2 %fusion = f32[1536,1024]{1,0:T(8,128)S(1)} fusion(f32[1,1,1536,1536]{3,2,1,0:T(8,128)} %param.6, f32[1,1,1536,1024]{3,2,1,0:T(8,128)} %param.7), kind=kOutput, calls=%fused_computation | convolution fusion | flops 14495514624 | bytes 22020096 | tf_op jit(solution)/shard_map/dot_general | solution.py:192
  23.7 0.0 slice-done
  23.7 0.0 copy-done.1
  23.7 0.0 slice-done.1
  23.7 11.6 %bitcast_subtract_fusion = f32[1024,1024]{0,1:T(8,128)} fusion(f32[1,1,1024,1024]{2,3,1,0:T(8,128)S(1)} %copy-done.1, f32[1536,1024]{1,0:T(8,128)S(1)} %fusion, f32[1,1,1536,1024]{3,2,1,0:T(8,128)S(1)} %bitcast.28), kind=kOutput, calls=%fused_computation.5 | convolution fusion | flops 9664724992 | bytes 20971520 | tf_op jit(solution)/shard_map/dot_general | solution.py:193
  35.3 5.3 %copy.15 = f32[1024,1024]{1,0:T(8,128)} copy(f32[1024,1024]{0,1:T(8,128)} %bitcast_subtract_fusion) | data formatting | bytes 8388608 | tf_op jit(solution)/shard_map/sub | solution.py:195
  40.6 0.0 copy-start.4
  40.6 0.0 copy-start.2
  40.6 0.0 copy-start.3
  40.6 4.8 %copy.16 = f32[2,2,16,4,4,8,128]{6,5,4,3,2,1,0:T(8,128)} copy(f32[2,2,16,4,4,8,128]{6,5,0,4,2,1,3:T(8,128)} %bitcast.25) | data formatting | bytes 8388608 | tf_op jit(solution)/shard_map/transpose | solution.py:196
  45.4 0.0 copy-done.4
  45.5 0.0 copy-done.2
  45.5 0.0 copy-done.3
  45.5 0.2 select_reduce_fusion.2
  45.7 0.1 pad_add_fusion
  45.7 0.1 fusion.7
  45.8 0.1 broadcast_in_dim.48
  45.9 0.1 select_reduce_fusion
  46.0 0.0 copy-start
  46.0 2.2 %copy-done = f32[2,2,16,4,4,8,128]{6,5,4,3,2,1,0:T(8,128)S(1)} copy-done((f32[2,2,16,4,4,8,128]{6,5,4,3,2,1,0:T(8,128)S(1)}, f32[2,2,16,4,4,8,128]{6,5,4,3,2,1,0:T(8,128)}, u32[]{:S(2)}) %copy-start) | copy-done | bytes 4194328
  48.2 82.3 %shard_map.64 = f32[2,256,256]{2,1,0:T(8,128)S(1)} custom-call(f32[4,16,4,4,8,128]{5,4,3,2,1,0:T(8,128)S(1)} %bitcast.23, s32[1,128]{1,0:T(1,128)S(1)} %select_bitcast_fusion.table), custom_call_target="tpu_custom_call" | custom-call | tf_op jit(solution)/shard_map/pallas_call | solution.py:211
  130.5 1.3 %copy.17 = f32[2,256,1,256]{3,2,1,0:T(1,128)} copy(f32[2,256,1,256]{3,1,0,2:T(8,128)S(1)} %bitcast.24) | data formatting | bytes 1048576 | tf_op jit(solution)/shard_map/broadcast_in_dim | solution.py:236
  (5 shorter events, 0.0 us)
Async XLA Ops:
  0.0 23.7 %slice-start = ((s8[6291456]{0:T(1024)(128)(4,1)}), s8[2097152]{0:T(1024)(128)(4,1)S(1)}, s32[]{:S(2)}) async-start(s8[6291456]{0:T(1024)(128)(4,1)} %bitcast.27), calls=%async_computation | async-start | bytes 4194304
  5.5 18.2 %copy-start.1 = (f32[1,1,1024,1024]{2,3,1,0:T(8,128)S(1)}, f32[1,1,1024,1024]{2,3,1,0:T(8,128)}, u32[]{:S(2)}) copy-start(f32[1,1,1024,1024]{2,3,1,0:T(8,128)} %copy.14) | copy-start | bytes 12582916
  5.5 18.2 %slice-start.1 = ((s8[6291456]{0:T(1024)(128)(4,1)}), s8[4194304]{0:T(1024)(128)(4,1)S(1)}, s32[]{:S(2)}) async-start(s8[6291456]{0:T(1024)(128)(4,1)} %bitcast.27), calls=%async_computation.1 | async-start | bytes 8388608
  40.6 4.8 %copy-start.4 = (s32[16]{0:T(128)S(1)}, s32[16]{0:T(128)}, u32[]{:S(2)}) copy-start(s32[16]{0:T(128)} %param.10) | copy-start | bytes 196
  40.6 4.8 %copy-start.2 = (s32[1,1,4]{2,1,0:T(1,128)S(1)}, s32[1,1,4]{2,1,0:T(1,128)}, u32[]{:S(2)}) copy-start(s32[1,1,4]{2,1,0:T(1,128)} %param.9) | copy-start | bytes 52
  40.6 4.8 %copy-start.3 = (s32[16]{0:T(128)S(1)}, s32[16]{0:T(128)}, u32[]{:S(2)}) copy-start(s32[16]{0:T(128)} %param.11) | copy-start | bytes 196
  46.0 2.2 %copy-start = (f32[2,2,16,4,4,8,128]{6,5,4,3,2,1,0:T(8,128)S(1)}, f32[2,2,16,4,4,8,128]{6,5,4,3,2,1,0:T(8,128)}, u32[]{:S(2)}) copy-start(f32[2,2,16,4,4,8,128]{6,5,4,3,2,1,0:T(8,128)} %copy.16) | copy-start | bytes 12582916
where the time goes:
time: 132 us
  Pallas kernels  82.3 us (62%)
  matrix products  29.7 us (22%)
  local copies, waits for them, and re-layouts  19.3 us (15%)
    pallas_call x1, Pallas kernels, on_device(): pl.pallas_call(kernel, out_shape=jax.ShapeDtypeStruct((2, 256, 256), f32)...  82.3 us
    dot_general x1, matrix products, on_device(): jnp.dot(inverse_interior[0, 0], coupling[0, 0], precision=high, preferred...  18.2 us
    dot_general x1, matrix products, on_device(): lax.dot_general(coupling[0, 0], solved, (((0,), (0,)), ((), ())), precisi...  11.6 us
    unnamed x15, local copies, waits for them, and re-layouts  7.71 us
    sub x1, local copies, waits for them, and re-layouts, on_device(): schur = interface_block[0, 0] - product  5.35 us
    transpose x1, local copies, waits for them, and re-layouts, on_device(): schur.reshape(4, 2, 16, 8, 4, 2, 128).transpose(5, 1, 2, 0, 4, 3, 6)  4.79 us

commit v1 on v0

--- a/solution.py
+++ b/solution.py
@@ -14,7 +14,7 @@
     (0, 1), (1, 0), (0, 3), (3, 0), (0, 2), (2, 0), (1, 1), (3, 3),
     (1, 3), (3, 1), (1, 2), (2, 1), (2, 3), (3, 2), (2, 2),
 )
-ROTATION = (0, 0, 0, 0)
+ROTATION = (0, 1, 2, 0)
 
 
 def plane_of(r, z, y, x):
@@ -25,7 +25,22 @@
     return ((w, u, v), (u, v, w), (v, w, u))[r]
 
 
-def kernel(pieces, table, out, arrived0, arrived1, arrived2, arrived3, table_in, table_s, give, take, grid, moved, done, final, zero_sem,
+def split(value):
+    high = value.astype(jnp.bfloat16)
+    return high, (value - high.astype(jnp.float32)).astype(jnp.bfloat16)
+
+
+def product(left_high, left_low, right_high, right_low):
+    def dot(left, right):
+        return jnp.dot(left, right, preferred_element_type=jnp.float32)
+
+    return dot(left_high, right_high) + (dot(left_high, right_low) + dot(left_low, right_high))
+
+
+def kernel(inverse, coupling, block, ids, row_place, col_place, out,
+           a_in, a_high, a_low, c_in, c_high, c_low, t_high, t_low, x_high, x_low, s_in, pieces, table,
+           arrived0, arrived1, arrived2, arrived3, table_in, table_s, give, take, grid, moved, done, final,
+           a_sem, c_sem, s_sem, zero_sem,
            data_s, data_r, tab_s, tab_r, own_sem, sib_s, sib_r, mov_s, mov_r, fin_s, fin_r):
     row, col = lax.axis_index("row"), lax.axis_index("col")
     z, core = row // 2, row % 2
@@ -60,21 +75,47 @@
                             device_id_type=MESH)
     pl.semaphore_signal(barrier, inc=1, device_id=sibling, device_id_type=MESH)
 
+    blocks, slots, depth = 6, a_in.shape[0], 256
+
+    def load_a(m):
+        return pltpu.make_async_copy(
+            inverse.at[0, 0, pl.ds(m * depth, depth), :], a_in.at[m % slots], a_sem.at[m % slots])
+
+    def load_c(h):
+        return [pltpu.make_async_copy(
+            coupling.at[0, 0, :, pl.ds(b * 256 + h * 128, 128)], c_in.at[:, pl.ds(b * 128, 128)], c_sem.at[h, b])
+            for b in range(4)]
+
+    def load_s(h):
+        return [pltpu.make_async_copy(
+            block.at[0, 0, :, pl.ds(b * 256 + h * 128, 128)], s_in.at[h, :, pl.ds(b * 128, 128)], s_sem.at[h, b])
+            for b in range(4)]
+
+    c_loads = {h: load_c(h) for h in range(2)}
+    s_loads = {h: load_s(h) for h in range(2)}
+    a_loads = [load_a(m) for m in range(blocks)]
+    for copy in c_loads[0]:
+        copy.start()
+    for m in range(slots):
+        a_loads[m].start()
+    for copy in s_loads[0] + s_loads[1]:
+        copy.start()
+
+    lane = lax.broadcasted_iota(jnp.int32, (1, 128), 1)
+    value = jnp.full((1, 128), 4, jnp.int32)
+    for k in range(4):
+        g = ids[0, 0, k]
+        rp, cp = row_place[g], col_place[g]
+        value = jnp.where(lane == (rp & 7) * 2 + (rp >> 3), k, value)
+        value = jnp.where(lane == 16 + (cp & 15) + (cp >> 4), k, value)
+    table[...] = value
     for c in chunks:
         arrived[c][:, 4, :] = jnp.zeros((16, 5, 8, 128), jnp.float32)
         arrived[c][:, :, 4] = jnp.zeros((16, 5, 8, 128), jnp.float32)
-    pl.semaphore_wait(barrier, len(offsets) + 1)
-
-    waits = []
+
     table_copies, data_copies = {}, {}
-    for n, r in enumerate(rotations):
-        for k, (du, dv) in enumerate(ORDER):
-            copy = pltpu.make_async_remote_copy(
-                src_ref=table, dst_ref=table_in.at[n, place(r)], send_sem=tab_s.at[n, k],
-                recv_sem=tab_r.at[n, k], device_id=member(r, du, dv), device_id_type=MESH)
-            copy.start()
-            table_copies[n, k] = copy
-    for c in chunks:
+
+    def send(c):
         r = ROTATION[c]
         for k, (du, dv) in enumerate(ORDER):
             copy = pltpu.make_async_remote_copy(
@@ -83,12 +124,85 @@
                 device_id=member(r, du, dv), device_id_type=MESH)
             copy.start()
             data_copies[c, k] = copy
-    own_copies = []
-    for c in chunks:
-        p = place(ROTATION[c])
+        p = place(r)
         copy = pltpu.make_async_copy(pieces.at[c, p], arrived[c].at[p, pl.ds(0, 4), pl.ds(0, 4)], own_sem.at[c])
         copy.start()
-        own_copies.append(copy)
+        own_copies[c] = copy
+
+    def prepare_c(h):
+        for copy in c_loads[h]:
+            copy.wait()
+
+        def body(n, carry):
+            rows = pl.ds(pl.multiple_of(n * 128, 128), 128)
+            value = c_in[rows, :]
+            c_high[h, rows, :], c_low[h, rows, :] = split(value)
+            t_high[h, :, rows], t_low[h, :, rows] = split(value.T)
+            return carry
+
+        lax.fori_loop(0, 12, body, 0)
+
+    def solve(h, m):
+        rows = pl.ds(m * depth, depth)
+        if h == 0:
+            a_loads[m].wait()
+            a_high[rows, :], a_low[rows, :] = split(a_in[m % slots])
+            if m + slots < blocks:
+                a_loads[m + slots].start()
+
+        def body(n, carry):
+            cols = pl.ds(pl.multiple_of(n * 256, 256), 256)
+            x_high[rows, cols], x_low[rows, cols] = split(
+                product(a_high[rows, :], a_low[rows, :], c_high[h, :, cols], c_low[h, :, cols]))
+            return carry
+
+        lax.fori_loop(0, 2, body, 0)
+
+    def finish(h, q):
+        c = h * 2 + q
+
+        def body(n, carry):
+            cols = pl.ds(pl.multiple_of(n * 256, 256), 256)
+            value = product(t_high[q], t_low[q], x_high[:, cols], x_low[:, cols])
+            for a in range(4):
+                for b in range(2):
+                    mine = s_in[h, a * 256 + q * 128:a * 256 + q * 128 + 128,
+                                pl.ds(pl.multiple_of(n * 256 + b * 128, 128), 128)]
+                    tile = mine - value[a * 128:(a + 1) * 128, b * 128:(b + 1) * 128]
+                    pieces[c, :, a, n * 2 + b] = tile.reshape(16, 8, 128)
+            return carry
+
+        lax.fori_loop(0, 2, body, 0)
+
+    own_copies = {}
+    prepare_c(0)
+    for copy in c_loads[1]:
+        copy.start()
+    for m in range(blocks):
+        solve(0, m)
+    for copy in s_loads[0]:
+        copy.wait()
+    pl.semaphore_wait(barrier, len(offsets) + 1)
+    finish(0, 0)
+    send(0)
+    for n, r in enumerate(rotations):
+        for k, (du, dv) in enumerate(ORDER):
+            copy = pltpu.make_async_remote_copy(
+                src_ref=table, dst_ref=table_in.at[n, place(r)], send_sem=tab_s.at[n, k],
+                recv_sem=tab_r.at[n, k], device_id=member(r, du, dv), device_id_type=MESH)
+            copy.start()
+            table_copies[n, k] = copy
+    prepare_c(1)
+    finish(0, 1)
+    send(1)
+    for m in range(blocks):
+        solve(1, m)
+    for copy in s_loads[1]:
+        copy.wait()
+    finish(1, 0)
+    send(2)
+    finish(1, 1)
+    send(3)
     for n, r in enumerate(rotations):
         table_in[n, place(r)] = table[...]
     for n, r in enumerate(rotations):
@@ -188,32 +302,25 @@
 
 
 def on_device(inverse_interior, coupling, interface_block, iface_ids, row_place, col_place):
-    high = lax.Precision.HIGH
-    solved = jnp.dot(inverse_interior[0, 0], coupling[0, 0], precision=high, preferred_element_type=jnp.float32)
-    product = lax.dot_general(coupling[0, 0], solved, (((0,), (0,)), ((), ())), precision=high,
-                              preferred_element_type=jnp.float32)
-    schur = interface_block[0, 0] - product
-    pieces = schur.reshape(4, 2, 16, 8, 4, 2, 128).transpose(5, 1, 2, 0, 4, 3, 6).reshape(4, 16, 4, 4, 8, 128)
-    ids = iface_ids[0, 0]
-    rowpos = (row_place % 8) * 2 + row_place // 8
-    matches = ids[:, None] == jnp.arange(16, dtype=jnp.int32)[None, :]
-    rows = jnp.sum(jnp.where(matches, rowpos[None, :], 0), axis=1)
-    cols = jnp.sum(jnp.where(matches, col_place[None, :], 0), axis=1)
-    lane = jnp.arange(128, dtype=jnp.int32)
-    wanted = jnp.concatenate([rows, cols + 16]).astype(jnp.int32)
-    value = jnp.tile(jnp.arange(4, dtype=jnp.int32), 2)
-    hit = wanted[:, None] == lane[None, :]
-    table = jnp.where(jnp.any(hit, axis=0), jnp.sum(jnp.where(hit, value[:, None], 0), axis=0), 4)[None, :]
     chunks, planes = len(ROTATION), len(set(ROTATION))
-    f32 = jnp.float32
+    f32, bf16 = jnp.float32, jnp.bfloat16
     vmem = pl.BlockSpec(memory_space=pltpu.VMEM)
     dma = pltpu.SemaphoreType.DMA
     out = pl.pallas_call(
         kernel,
         out_shape=jax.ShapeDtypeStruct((2, 256, 256), f32),
-        in_specs=[pl.BlockSpec(memory_space=pl.ANY), vmem],
+        in_specs=[pl.BlockSpec(memory_space=pl.ANY)] * 3 + [pl.BlockSpec(memory_space=pltpu.SMEM)] * 3,
         out_specs=vmem,
         scratch_shapes=[
+            pltpu.VMEM((4, 256, 1536), f32),
+            *[pltpu.VMEM((1536, 1536), bf16)] * 2,
+            pltpu.VMEM((1536, 512), f32),
+            *[pltpu.VMEM((2, 1536, 512), bf16)] * 2,
+            *[pltpu.VMEM((2, 512, 1536), bf16)] * 2,
+            *[pltpu.VMEM((1536, 512), bf16)] * 2,
+            pltpu.VMEM((2, 1024, 512), f32),
+            pltpu.VMEM((chunks, 16, 4, 4, 8, 128), f32),
+            pltpu.VMEM((1, 128), jnp.int32),
             *[pltpu.VMEM((16, 5, 5, 8, 128), f32)] * chunks,
             pltpu.VMEM((planes, 16, 1, 128), jnp.int32),
             pltpu.SMEM((planes, 16, 1, 128), jnp.int32),
@@ -223,7 +330,7 @@
             pltpu.VMEM((chunks, 3, 16, 2, 8, 128), f32),
             pltpu.VMEM((chunks, 16, 2, 8, 128), f32),
             pltpu.VMEM((2, 256, 256), f32),
-            dma,
+            dma((4,)), dma((2, 4)), dma((2, 4)), dma,
             dma((chunks, 15)), dma((chunks, 15)),
             dma((planes, 15)), dma((planes, 15)),
             dma((chunks,)),
@@ -231,8 +338,8 @@
             dma((chunks, 3)), dma((chunks, 3)),
             dma((chunks, 15)), dma((chunks, 15)),
         ],
-        compiler_params=pltpu.CompilerParams(collective_id=0, has_side_effects=True, vmem_limit_bytes=48 * 2**20),
-    )(pieces, table)
+        compiler_params=pltpu.CompilerParams(collective_id=0, has_side_effects=True, vmem_limit_bytes=60 * 2**20),
+    )(inverse_interior, coupling, interface_block, iface_ids, row_place, col_place)
     return out[:, :, None, :]
 
 

time: 132 us -> 99.6 us (0.75)
  matrix products: 29.7 us -> 0 us
  local copies, waits for them, and re-layouts: 19.3 us -> 2.37 us
  Pallas kernels: 82.3 us -> 97 us
    dot_general x2 -> x0, matrix products: 29.7 us -> none  [the longest x1 18.2 us: on_device(): jnp.dot(inverse_interior[0, 0], coupling[0, 0], precision=high, preferred...]
    pallas_call x1, Pallas kernels: 82.3 us -> 97 us  [on_device(): pl.pallas_call(kernel, out_shape=jax.ShapeDtypeStruct((2, 256, 256), f32)...]
    unnamed x15 -> x0, local copies, waits for them, and re-layouts: 7.71 us -> none
    sub x1 -> x0, local copies, waits for them, and re-layouts: 5.35 us -> none  [on_device(): schur = interface_block[0, 0] - product]
    transpose x1 -> x0, local copies, waits for them, and re-layouts: 4.79 us -> none  [on_device(): schur.reshape(4, 2, 16, 8, 4, 2, 128).transpose(5, 1, 2, 0, 4, 3, 6)]
where the time goes in v1:
time: 99.6 us; the launch traced here: 99.4 us
  Pallas kernels  97 us (97%)
  local copies, waits for them, and re-layouts  2.37 us (2%)
    pallas_call x1, Pallas kernels, on_device(): pl.pallas_call(kernel, out_shape=jax.ShapeDtypeStruct((2, 256, 256), f32)...  97 us
    broadcast_in_dim x1, local copies, waits for them, and re-layouts, on_device(): return out[:, :, None, :]  2.37 us

profile of v1, /device:TPU:0, one launch (start us, length us, event | category | flops | bytes accessed | tf_op | source)
XLA Modules:
  0.0 99.4 jit_solution(5134689900199965545)
XLA Ops:
  0.0 97.0 %shard_map.64 = f32[2,256,256]{2,1,0:T(8,128)} custom-call(f32[1,1,1536,1536]{3,2,1,0:T(8,128)} %inverse.1, f32[1,1,1536,1024]{3,2,1,0:T(8,128)} %coupling.1, f32[1,1,1024,1024]{3,2,1,0:T(8,128)} %block.1, s32[1,1,4]{2,1,0:T(1,128)} %ids.1, s32[16]{0:T(128)} %row_place.1, s32[16]{0:T(128)} %col_place.1), custom_call_target="tpu_custom_call" | custom-call | tf_op jit(solution)/shard_map/pallas_call | solution.py:309
  97.0 2.4 %copy.7 = f32[2,256,1,256]{3,2,1,0:T(1,128)} copy(f32[2,256,1,256]{3,1,0,2:T(8,128)} %bitcast.1) | data formatting | bytes 1048576 | tf_op jit(solution)/shard_map/broadcast_in_dim | solution.py:343

commit v2 on v0

v2 whole, which is shorter than its diff:
```python
import functools

import jax
import jax.numpy as jnp
from jax import lax
from jax.experimental import pallas as pl
from jax.experimental.pallas import tpu as pltpu
from jax.sharding import PartitionSpec as P

TILE = 256
MESH = pl.DeviceIdType.MESH

ORDER = (
    (0, 1), (1, 0), (0, 3), (3, 0), (0, 2), (2, 0), (1, 1), (3, 3),
    (1, 3), (3, 1), (1, 2), (2, 1), (2, 3), (3, 2), (2, 2),
)
ROTATION = (0, 0, 0, 0)


def plane_of(r, z, y, x):
    return ((y, x, z), (z, y, x), (x, z, y))[r]


def chip_of(r, u, v, w):
    return ((w, u, v), (u, v, w), (v, w, u))[r]


STRIDE = 33


def split(value):
    high = value.astype(jnp.bfloat16)
    return high, (value - high.astype(jnp.float32)).astype(jnp.bfloat16)


def product(left_high, left_low, right_high, right_low):
    def dot(left, right):
        return jnp.dot(left, right, preferred_element_type=jnp.float32)

    return dot(left_high, right_high) + (dot(left_high, right_low) + dot(left_low, right_high))


def kernel(inverse, coupling, block, ids, row_place, col_place, out,
           a_in, a_high, a_low, c_in, c_high, c_low, t_high, t_low, x_high, x_low, s_in, pieces, table,
           arrived0, arrived1, arrived2, arrived3, table_in, table_s, give, take, grid, moved, done, final,
           a_sem, c_sem, s_sem, lab_sem,
           data_s, data_r, tab_s, tab_r, own_sem, sib_s, sib_r, mov_s, mov_r, fin_s, fin_r):
    row, col = lax.axis_index("row"), lax.axis_index("col")
    z, core = row // 2, row % 2
    y, x = col // 4, col % 4
    arrived = (arrived0, arrived1, arrived2, arrived3)
    chunks = range(len(ROTATION))
    rotations = sorted(set(ROTATION))

    def device(zz, yy, xx, cc=None):
        return (zz * 2 + (core if cc is None else cc), yy * 4 + xx)

    def member(r, du, dv, dw=0):
        u, v, w = plane_of(r, z, y, x)
        return device(*chip_of(r, (u + du) % 4, (v + dv) % 4, (w + dw) % 4))

    def place(r, du=0, dv=0):
        u, v, _ = plane_of(r, z, y, x)
        return ((u + du) % 4) * 4 + (v + dv) % 4

    sibling = device(z, y, x, 1 - core)
    blocks, slots, depth = 6, a_in.shape[0], 256

    def load_a(m):
        return pltpu.make_async_copy(
            inverse.at[0, 0, pl.ds(m * depth, depth), :], a_in.at[m % slots], a_sem.at[m % slots])

    def load_c(h, b):
        return pltpu.make_async_copy(
            coupling.at[0, 0, :, pl.ds(b * 256 + h * 128, 128)], c_in.at[h, :, pl.ds(b * 128, 128)], c_sem.at[h, b])

    def load_s(h, b):
        return pltpu.make_async_copy(
            block.at[0, 0, :, pl.ds(b * 256 + h * 128, 128)], s_in.at[h, :, pl.ds(b * 128, 128)], s_sem.at[h, b])

    a_loads = [load_a(m) for m in range(blocks)]
    c_loads = [[load_c(h, b) for b in range(4)] for h in range(2)]
    s_loads = [[load_s(h, b) for b in range(4)] for h in range(2)]
    for copy in c_loads[0]:
        copy.start()
    for m in range(slots):
        a_loads[m].start()

    offsets = set()
    for r in rotations:
        for du, dv in ORDER:
            offsets.add(chip_of(r, du, dv, 0))
        for dw in (1, 2, 3):
            offsets.add(chip_of(r, 0, 0, dw))
    offsets = sorted(offsets)
    barrier = pltpu.get_barrier_semaphore()
    for dz, dy, dx in offsets:
        pl.semaphore_signal(barrier, inc=1, device_id=device((z + dz) % 4, (y + dy) % 4, (x + dx) % 4),
                            device_id_type=MESH)
    pl.semaphore_signal(barrier, inc=1, device_id=sibling, device_id_type=MESH)

    lane = lax.broadcasted_iota(jnp.int32, (1, 128), 1)
    value = jnp.full((1, 128), 16, jnp.int32)
    for k in range(4):
        g = ids[0, 0, k]
        rp, cp = row_place[g], col_place[g]
        value = jnp.where(lane == (rp & 7) * 2 + (rp >> 3), k * 2, value)
        value = jnp.where(lane == 16 + (cp & 15) + (cp >> 4), (k // 2) * 8 + k % 2, value)
    table[...] = value
    for c in chunks:
        for n in range(16):
            arrived[c][n * STRIDE + 16:(n + 1) * STRIDE] = jnp.zeros((STRIDE - 16, 8, 128), jnp.float32)

    def prepare_c(h):
        for copy in c_loads[h]:
            copy.wait()

        def body(n, carry):
            rows = pl.ds(pl.multiple_of(n * 128, 128), 128)
            value = c_in[h, rows, :]
            c_high[h, rows, :], c_low[h, rows, :] = split(value)
            t_high[h, :, rows], t_low[h, :, rows] = split(value.T)
            return carry

        lax.fori_loop(0, 12, body, 0)

    def solve_first(m):
        rows = pl.ds(m * depth, depth)
        a_loads[m].wait()
        a_high[rows, :], a_low[rows, :] = split(a_in[m % slots])
        if m + slots < blocks:
            a_loads[m + slots].start()
        x_high[0, rows, :], x_low[0, rows, :] = split(
            product(a_high[rows, :], a_low[rows, :], c_high[0, :, 0:256], c_low[0, :, 0:256]))

    def solve(h, pair):
        cols = slice(pair * 256, pair * 256 + 256)

        def body(m, carry):
            rows = pl.ds(pl.multiple_of(m * 512, 512), 512)
            x_high[pair, rows, :], x_low[pair, rows, :] = split(
                product(a_high[rows, :], a_low[rows, :], c_high[h, :, cols], c_low[h, :, cols]))
            return carry

        lax.fori_loop(0, 3, body, 0)

    def finish(h, pair, q):
        value = product(t_high[q], t_low[q], x_high[pair], x_low[pair])
        for a in range(4):
            for b in range(2):
                mine = s_in[h, a * 256 + q * 128:a * 256 + q * 128 + 128,
                            pair * 256 + b * 128:pair * 256 + b * 128 + 128]
                tile = mine - value[a * 128:(a + 1) * 128, b * 128:(b + 1) * 128]
                pieces[h * 2 + q, :, pair * 8 + a * 2 + b] = tile.reshape(16, 8, 128)

    table_copies, data_copies, own_copies = {}, {}, {}

    def parts(c):
        return (0, 1) if c < 2 else (2,)

    def send(h, part, q):
        c = h * 2 + q
        r = ROTATION[c]
        p = place(r)
        start, size = (0, 16) if part == 2 else (part * 8, 8)
        target = arrived[c].at[pl.ds(p * STRIDE + start, size)]
        for k, (du, dv) in enumerate(ORDER):
            copy = pltpu.make_async_remote_copy(
                src_ref=pieces.at[c, place(r, du, dv), pl.ds(start, size)], dst_ref=target,
                send_sem=data_s.at[c, part % 2, k], recv_sem=data_r.at[c, part % 2, k],
                device_id=member(r, du, dv), device_id_type=MESH)
            copy.start()
            data_copies[c, part, k] = copy
        copy = pltpu.make_async_copy(pieces.at[c, p, pl.ds(start, size)], target, own_sem.at[c, part % 2])
        copy.start()
        own_copies[c, part] = copy

    def send_tables():
        for n, r in enumerate(rotations):
            for k, (du, dv) in enumerate(ORDER):
                copy = pltpu.make_async_remote_copy(
                    src_ref=table, dst_ref=table_in.at[n, place(r)], send_sem=tab_s.at[n, k],
                    recv_sem=tab_r.at[n, k], device_id=member(r, du, dv), device_id_type=MESH)
                copy.start()
                table_copies[n, k] = copy
            table_in[n, place(r)] = table[...]

    prepare_c(0)
    for m in range(blocks):
        solve_first(m)
        if m == 1:
            for copy in s_loads[0] + c_loads[1] + s_loads[1]:
                copy.start()
        if m == 3:
            pl.semaphore_wait(barrier, len(offsets) + 1)
            send_tables()
    for copy in s_loads[0]:
        copy.wait()
    finish(0, 0, 0)
    send(0, 0, 0)
    prepare_c(1)
    finish(0, 0, 1)
    send(0, 0, 1)
    solve(0, 1)
    finish(0, 1, 0)
    send(0, 1, 0)
    finish(0, 1, 1)
    send(0, 1, 1)
    for copy in s_loads[1]:
        copy.wait()
    for pair in range(2):
        solve(1, pair)
    for q in range(2):
        for pair in range(2):
            finish(1, pair, q)
        send(1, 2, q)

    for copy in table_copies.values():
        copy.wait()
    copy = pltpu.make_async_copy(table_in, table_s, lab_sem)
    copy.start()
    copy.wait()

    fin_copies = {}

    def total(c, zz, who):
        first = zz * 4 + who * 2
        acc = [[None] * 16 for _ in range(2)]
        for s in range(16):
            ra = [table_s[0, s, 0, first + slot] for slot in range(2)]
            for j in range(16):
                cb = table_s[0, s, 0, 16 + j]
                for slot in range(2):
                    piece = arrived[c][ra[slot] + cb + s * STRIDE]
                    acc[slot][j] = piece if s == 0 else acc[slot][j] + piece
        return acc

    def sib_copy(c, zz):
        return pltpu.make_async_remote_copy(
            src_ref=give.at[c, zz], dst_ref=take.at[c, zz], send_sem=sib_s.at[c, zz], recv_sem=sib_r.at[c, zz],
            device_id=sibling, device_id_type=MESH)

    def mov_copy(c, dw):
        there = (z + dw) % 4
        return pltpu.make_async_remote_copy(
            src_ref=grid.at[c, there], dst_ref=moved.at[c, dw - 1], send_sem=mov_s.at[c, dw - 1],
            recv_sem=mov_r.at[c, dw - 1], device_id=device(there, y, x), device_id_type=MESH)

    def stage_reduce(c):
        for part in parts(c):
            for k in range(15):
                data_copies[c, part, k].wait_recv()
            own_copies[c, part].wait()

        def other(n, carry):
            zz = (z + 3 - n) % 4
            acc = total(c, zz, 1 - core)
            for j in range(16):
                for slot in range(2):
                    give[c, zz, j, slot] = acc[slot][j]
            sib_copy(c, zz).start()
            return carry

        def mine(n, carry):
            zz = (z + 3 - n) % 4
            acc = total(c, zz, core)
            sib_copy(c, zz).wait_recv()
            for j in range(16):
                for slot in range(2):
                    grid[c, zz, j, slot] = acc[slot][j] + take[c, zz, j, slot]

            @pl.when(n < 3)
            def _():
                mov_copy(c, 3 - n).start()

            return carry

        lax.fori_loop(0, 4, other, 0)
        lax.fori_loop(0, 4, mine, 0)

    def stage_final(c):
        r = ROTATION[c]
        _, _, w = plane_of(r, z, y, x)
        h, q = c // 2, c % 2
        for dw in (1, 2, 3):
            mov_copy(c, dw).wait_recv()
        done[c] = grid[c, w] + moved[c, 0] + moved[c, 1] + moved[c, 2]
        p = place(r)
        rows = pl.ds(pl.multiple_of(q * 128 + p * 8, 8), 8)
        for k, (du, dv) in enumerate(ORDER):
            copy = pltpu.make_async_remote_copy(
                src_ref=done.at[c, place(r, du, dv)], dst_ref=final.at[:, rows, pl.ds(h * 128, 128)],
                send_sem=fin_s.at[c, k], recv_sem=fin_r.at[c, k],
                device_id=member(r, du, dv), device_id_type=MESH)
            copy.start()
            fin_copies[c, k] = copy
        final[:, rows, h * 128:(h + 1) * 128] = done[c, p]

    last = len(ROTATION) - 1
    for step in range(last + 2):
        if step <= last:
            stage_reduce(step)
    for c in chunks:
        stage_final(c)
    for c in chunks:
        for k in range(15):
            fin_copies[c, k].wait_recv()
    out[...] = final[...]
    for c in chunks:
        for k in range(15):
            for part in parts(c):
                data_copies[c, part, k].wait_send()
            fin_copies[c, k].wait_send()
        for dw in (1, 2, 3):
            mov_copy(c, dw).wait_send()
        for zz in range(4):
            sib_copy(c, zz).wait_send()


def on_device(inverse_interior, coupling, interface_block, iface_ids, row_place, col_place):
    chunks, planes = len(ROTATION), len(set(ROTATION))
    f32, bf16 = jnp.float32, jnp.bfloat16
    vmem = pl.BlockSpec(memory_space=pltpu.VMEM)
    dma = pltpu.SemaphoreType.DMA
    out = pl.pallas_call(
        kernel,
        out_shape=jax.ShapeDtypeStruct((2, 256, 256), f32),
        in_specs=[pl.BlockSpec(memory_space=pl.ANY)] * 3 + [pl.BlockSpec(memory_space=pltpu.SMEM)] * 3,
        out_specs=vmem,
        scratch_shapes=[
            pltpu.VMEM((3, 256, 1536), f32),
            *[pltpu.VMEM((1536, 1536), bf16)] * 2,
            pltpu.VMEM((2, 1536, 512), f32),
            *[pltpu.VMEM((2, 1536, 512), bf16)] * 2,
            *[pltpu.VMEM((2, 512, 1536), bf16)] * 2,
            *[pltpu.VMEM((2, 1536, 256), bf16)] * 2,
            pltpu.VMEM((2, 1024, 512), f32),
            pltpu.VMEM((chunks, 16, 16, 8, 128), f32),
            pltpu.VMEM((1, 128), jnp.int32),
            *[pltpu.VMEM((16 * STRIDE, 8, 128), f32)] * chunks,
            pltpu.VMEM((planes, 16, 1, 128), jnp.int32),
            pltpu.SMEM((planes, 16, 1, 128), jnp.int32),
            pltpu.VMEM((chunks, 4, 16, 2, 8, 128), f32),
            pltpu.VMEM((chunks, 4, 16, 2, 8, 128), f32),
            pltpu.VMEM((chunks, 4, 16, 2, 8, 128), f32),
            pltpu.VMEM((chunks, 3, 16, 2, 8, 128), f32),
            pltpu.VMEM((chunks, 16, 2, 8, 128), f32),
            pltpu.VMEM((2, 256, 256), f32),
            dma((4,)), dma((2, 4)), dma((2, 4)), dma,
            dma((chunks, 2, 15)), dma((chunks, 2, 15)),
            dma((planes, 15)), dma((planes, 15)),
            dma((chunks, 2)),
            dma((chunks, 4)), dma((chunks, 4)),
            dma((chunks, 3)), dma((chunks, 3)),
            dma((chunks, 15)), dma((chunks, 15)),
        ],
        compiler_params=pltpu.CompilerParams(collective_id=0, has_side_effects=True, vmem_limit_bytes=62 * 2**20),
    )(inverse_interior, coupling, interface_block, iface_ids, row_place, col_place)
    return out[:, :, None, :]


def solution(mesh):
    return jax.shard_map(
        on_device,
        mesh=mesh,
        in_specs=(
            P("row", "col", None, None),
            P("row", "col", None, None),
            P("row", "col", None, None),
            P("row", "col", None),
            P(),
            P(),
        ),
        out_specs=P("row", None, "col", None),
        check_vma=False,
    )
```

time: 132 us -> 96.1 us (0.73)
  matrix products: 29.7 us -> 0 us
  local copies, waits for them, and re-layouts: 19.3 us -> 2.37 us
  Pallas kernels: 82.3 us -> 93.6 us
    dot_general x2 -> x0, matrix products: 29.7 us -> none  [the longest x1 18.2 us: on_device(): jnp.dot(inverse_interior[0, 0], coupling[0, 0], precision=high, preferred...]
    pallas_call x1, Pallas kernels: 82.3 us -> 93.6 us  [on_device(): pl.pallas_call(kernel, out_shape=jax.ShapeDtypeStruct((2, 256, 256), f32)...]
    unnamed x15 -> x0, local copies, waits for them, and re-layouts: 7.71 us -> none
    sub x1 -> x0, local copies, waits for them, and re-layouts: 5.35 us -> none  [on_device(): schur = interface_block[0, 0] - product]
    transpose x1 -> x0, local copies, waits for them, and re-layouts: 4.79 us -> none  [on_device(): schur.reshape(4, 2, 16, 8, 4, 2, 128).transpose(5, 1, 2, 0, 4, 3, 6)]
where the time goes in v2:
time: 96.1 us; the launch traced here: 96 us
  Pallas kernels  93.6 us (97%)
  local copies, waits for them, and re-layouts  2.37 us (2%)
    pallas_call x1, Pallas kernels, on_device(): pl.pallas_call(kernel, out_shape=jax.ShapeDtypeStruct((2, 256, 256), f32)...  93.6 us
    broadcast_in_dim x1, local copies, waits for them, and re-layouts, on_device(): return out[:, :, None, :]  2.37 us

profile of v2, /device:TPU:0, one launch (start us, length us, event | category | flops | bytes accessed | tf_op | source)
XLA Modules:
  0.0 96.0 jit_solution(2522066091877814205)
XLA Ops:
  0.0 93.6 %shard_map.64 = f32[2,256,256]{2,1,0:T(8,128)} custom-call(f32[1,1,1536,1536]{3,2,1,0:T(8,128)} %inverse.1, f32[1,1,1536,1024]{3,2,1,0:T(8,128)} %coupling.1, f32[1,1,1024,1024]{3,2,1,0:T(8,128)} %block.1, s32[1,1,4]{2,1,0:T(1,128)} %ids.1, s32[16]{0:T(128)} %row_place.1, s32[16]{0:T(128)} %col_place.1), custom_call_target="tpu_custom_call" | custom-call | tf_op jit(solution)/shard_map/pallas_call | solution.py:325
  93.6 2.4 %copy.7 = f32[2,256,1,256]{3,2,1,0:T(1,128)} copy(f32[2,256,1,256]{3,1,0,2:T(8,128)} %bitcast.1) | data formatting | bytes 1048576 | tf_op jit(solution)/shard_map/broadcast_in_dim | solution.py:359
